TPU v7x, 32 devices: a whole 2x2x4 slice. The times are simulated.
32 devices in a mesh: batch: 8 (over z, core), seq: 4 (over y, x).
Axes of the slice: x: 2, y: 2, z: 4, core: 2. Of those that a mesh axis runs over, the one named last changes fastest.
Arguments:
- token_cond: bfloat16 [16384, 768], P(('batch', 'seq')), parts along dimension 0, may hold values from -6 to 6
- atom_feat: bfloat16 [131072, 128], P(('batch', 'seq')), parts along dimension 0, may hold values from -16 to 16
- atom_counts: int32 [16384], P(('batch', 'seq')), parts along dimension 0, may hold values from 1 to 24, as said below
- w_token: bfloat16 [768, 128], replicated, may hold values from -0.21875 to 0.21875
- w_query: bfloat16 [128, 128], replicated, may hold values from -0.5 to 0.5
- w_key: bfloat16 [128, 128], replicated, may hold values from -0.5 to 0.5
- w_value: bfloat16 [128, 128], replicated, may hold values from -0.5 to 0.5
- w_out: bfloat16 [128, 128], replicated, may hold values from -0.5 to 0.5
- w_back: bfloat16 [128, 768], replicated, may hold values from -0.5 to 0.5
Outputs:
- token_out: bfloat16 [16384, 768], P(('batch', 'seq')), parts along dimension 0
- atom_out: bfloat16 [131072, 128], P(('batch', 'seq')), parts along dimension 0
There are 8 independent parts, one for each index of `batch`. A program takes and returns all parts, laid end to end along the dimension named above; an argument that names none is the same for every part. Nothing has to cross between parts.
Inputs may be any that keep to these rules, and one draw needn't show every extreme that they name: `atom_counts`: every token has at least one atom and the counts of one complex sum to 16384. For every k, the atoms k * 4096 to (k + 1) * 4096 - 1 belong to tokens of (k - 1) * 512 to (k + 2) * 512 - 1.
All inputs are finite; a program needn't handle non-finite values.
Results may differ from a plain program's by a relative error of at most 0.0095.
The roundings to bfloat16 on the way count: a program that leaves them out, or rounds other values in their place, can miss the bound.
Values may be sent and summed in bfloat16 or wider, within the bound.
A program may use at most 128 MiB of HBM per device.

v0:
```python
import functools
import math

import jax
import jax.numpy as jnp
from jax import lax
from jax.experimental import pallas as pl
from jax.experimental.pallas import tpu as pltpu
from jax.sharding import PartitionSpec as P

HEADS = 4
QBLOCK = 32
KEYS = 128
HALO = 48
LANES = 128
MESH = pl.DeviceIdType.MESH
F32 = jnp.float32
BF16 = jnp.bfloat16


def dot(a, b, dims=((1,), (0,))):
    return lax.dot_general(a, b, (dims, ((), ())), preferred_element_type=F32)


def greet(n, me):
    barrier = pltpu.get_barrier_semaphore()
    for d in range(1, n):
        pl.semaphore_signal(barrier, inc=1, device_id={"seq": lax.rem(me + d, n)}, device_id_type=MESH)
    pl.semaphore_wait(barrier, n - 1)


def spread(n, atom_rows, cond_ref, wtok_ref, feat_ref, counts_ref, table_ref, halo_ref, ends_ref, starts_ref,
           proj, zeros, cnt, padded, ends_all, send_sem, recv_sem, csend, crecv, lsem):
    me = lax.axis_index("seq")
    tok = cond_ref.shape[0]
    crow = tok // LANES
    right, left = lax.rem(me + 1, n), lax.rem(me + n - 1, n)
    right2, left2 = lax.rem(me + 2, n), lax.rem(me + n - 2, n)

    def remote(i, src, dst, dev):
        return pltpu.make_async_remote_copy(
            src_ref=src, dst_ref=dst, send_sem=send_sem.at[i], recv_sem=recv_sem.at[i],
            device_id={"seq": dev}, device_id_type=MESH)

    greet(n, me)
    ccopies = []
    for d in range(1, n):
        c = pltpu.make_async_remote_copy(
            src_ref=counts_ref, dst_ref=cnt.at[d - 1], send_sem=csend.at[d - 1], recv_sem=crecv.at[d - 1],
            device_id={"seq": lax.rem(me + d, n)}, device_id_type=MESH)
        c.start()
        ccopies.append(c)
    copies = [
        remote(0, feat_ref.at[pl.ds(atom_rows - HALO, HALO)], halo_ref.at[pl.ds(0, HALO)], right),
        remote(1, feat_ref.at[pl.ds(0, HALO)], halo_ref.at[pl.ds(HALO, HALO)], left),
    ]
    for c in copies:
        c.start()
    proj[...] = dot(cond_ref[...], wtok_ref[...]).astype(BF16)
    more = [
        remote(2, proj, table_ref.at[pl.ds(LANES, tok)], right),
        remote(3, proj, table_ref.at[pl.ds(LANES + 2 * tok, tok)], left),
        remote(4, proj.at[pl.ds(tok - LANES, LANES)], table_ref.at[pl.ds(0, LANES)], right2),
        remote(5, proj.at[pl.ds(0, LANES)], table_ref.at[pl.ds(LANES + 3 * tok, LANES)], left2),
    ]
    for c in more:
        c.start()
    zeros[...] = jnp.zeros_like(zeros)
    own = pltpu.make_async_copy(proj, table_ref.at[pl.ds(LANES + tok, tok)], lsem.at[0])
    own.start()
    tail = pltpu.make_async_copy(zeros, table_ref.at[pl.ds(2 * LANES + 3 * tok, LANES)], lsem.at[1])
    tail.start()

    padded[...] = jnp.zeros_like(padded)
    rows = padded.shape[0]
    for c in ccopies:
        c.wait()
    for j in range(n):
        part = jnp.where(me == j, counts_ref[...], 0)
        for d in range(1, n):
            part = jnp.where(lax.rem(me + n - d, n) == j, cnt[d - 1], part)
        padded[pl.ds(8 + crow * j, crow), :] = part
    counts = padded[...].astype(F32).astype(BF16)
    tri = (lax.broadcasted_iota(jnp.int32, (LANES, LANES), 0)
           <= lax.broadcasted_iota(jnp.int32, (LANES, LANES), 1)).astype(F32).astype(BF16)
    before = (lax.broadcasted_iota(jnp.int32, (rows, rows), 1)
              < lax.broadcasted_iota(jnp.int32, (rows, rows), 0)).astype(F32).astype(BF16)
    inner = dot(counts, tri)
    outer = jnp.sum(dot(before, counts), axis=1, keepdims=True)
    ends_all[...] = (inner + outer).astype(jnp.int32)
    near = pl.ds(8 - 1 - crow + crow * me, ends_ref.shape[0])
    ends = ends_all[near, :] - me * atom_rows
    ends_ref[...] = ends
    starts_ref[...] = ends - padded[near, :]
    for c in copies + more:
        c.wait()
    own.wait()
    tail.wait()


def atoms(n, ends_s, table, halo, feat, ends_v, starts_v, wqkv, wout, out, own, sides,
          xs, qs, ks, vs, mem, pool):
    me = lax.axis_index("seq")
    atom_rows, width = feat.shape
    tok = own.shape[0]
    head = width // HEADS
    nrow = ends_v.shape[0]
    scale = math.log2(math.e) / math.sqrt(head)
    tiles = atom_rows // LANES

    def window(first):
        w = jnp.int32(0)
        for r in range(nrow - 1):
            w += (ends_s[r, LANES - 1] <= first).astype(jnp.int32)
        return jnp.minimum(w, nrow - 3)

    def gather(first, f):
        r = f.shape[0]
        w = window(first)
        ids = first + lax.broadcasted_iota(jnp.int32, (r, LANES), 0)
        parts = []
        for s in range(2):
            lo = starts_v[pl.ds(w + s, 1), :]
            hi = ends_v[pl.ds(w + s, 1), :]
            parts.append(jnp.where((ids >= lo) & (ids < hi), F32(1), F32(0)).astype(BF16))
        member = jnp.concatenate(parts, axis=1)
        rows = dot(member, table[pl.ds(pl.multiple_of(w * LANES, LANES), 2 * LANES), :])
        x = (f.astype(F32) + rows).astype(BF16)
        return w, member, x

    def keyval(at, qkv, r):
        ks[pl.ds(at, r), :] = qkv[:, width:2 * width].astype(BF16)
        vs[pl.ds(at, r), :] = qkv[:, 2 * width:].astype(BF16)

    weights = wqkv[...]
    for first, at in ((-HALO, 0), (atom_rows, atom_rows + HALO)):
        f = halo[pl.ds(0 if first < 0 else HALO, HALO), :]
        _, _, x = gather(jnp.int32(first), f)
        keyval(at, dot(x, weights), HALO)

    def first_pass(i, c):
        for u in range(2):
            a = pl.multiple_of((2 * i + u) * LANES, LANES)
            _, member, x = gather(a, feat[pl.ds(a, LANES), :])
            mem[pl.ds(a, LANES), :] = member
            xs[pl.ds(a, LANES), :] = x
            qkv = dot(x, weights)
            qs[pl.ds(a, LANES), :] = qkv[:, :width].astype(BF16)
            keyval(pl.multiple_of(a + HALO, 16), qkv, LANES)
        return c

    lax.fori_loop(0, tiles // 2, first_pass, 0)

    pool[...] = jnp.zeros_like(pool)
    lane = lax.broadcasted_iota(jnp.int32, (1, width), 1)
    hmask = [((lane >= h * head) & (lane < (h + 1) * head)) for h in range(HEADS)]
    hmul = [jnp.where(m, F32(1), F32(0)).astype(BF16) for m in hmask]
    ones = jnp.ones((KEYS, width), BF16)
    total = atom_rows * n
    klane = lax.broadcasted_iota(jnp.int32, (1, KEYS), 1)
    per = LANES // QBLOCK
    group = 2

    def pick(o):
        r = o[(HEADS - 1) * QBLOCK:]
        for h in range(HEADS - 2, -1, -1):
            r = jnp.where(hmask[h], o[h * QBLOCK:(h + 1) * QBLOCK], r)
        return r

    def second_pass(i, c):
        base = i * group * LANES
        scores = []
        for j in range(group * per):
            at = pl.multiple_of(base + j * QBLOCK, QBLOCK)
            q = qs[pl.ds(at, QBLOCK), :]
            qb = jnp.concatenate([q * m for m in hmul], axis=0)
            s = dot(qb, ks[pl.ds(at, KEYS), :], ((1,), (1,)))
            pos = me * atom_rows + at - HALO + klane
            scores.append(jnp.where((pos >= 0) & (pos < total), s, F32(-1e30)))
        probs = []
        for s in scores:
            m = jnp.max(s, axis=1, keepdims=True)
            probs.append(jnp.exp2((s - m) * F32(scale)).astype(BF16))
        outs = []
        for j, p in enumerate(probs):
            at = pl.multiple_of(base + j * QBLOCK, QBLOCK)
            o = dot(p, jnp.concatenate([vs[pl.ds(at, KEYS), :], ones], axis=1))
            outs.append((pick(o[:, :width]) / pick(o[:, width:])).astype(BF16))
        for u in range(group):
            a = pl.multiple_of(base + u * LANES, LANES)
            att = jnp.concatenate(outs[u * per:(u + 1) * per], axis=0)
            y = (xs[pl.ds(a, LANES), :].astype(F32) + dot(att, wout[...])).astype(BF16)
            out[pl.ds(a, LANES), :] = y
            part = dot(mem[pl.ds(a, LANES), :], y, ((0,), (0,)))
            at = pl.ds(pl.multiple_of(window(a) * LANES, LANES), 2 * LANES)
            pool[at, :] += part
        return c

    lax.fori_loop(0, tiles // group, second_pass, 0)
    own[...] = pool[pl.ds(LANES + tok, tok), :]
    sides[0] = pool[pl.ds(LANES, tok), :].astype(BF16)
    sides[1] = pool[pl.ds(LANES + 2 * tok, tok), :].astype(BF16)


def merge(n, own_ref, sides_ref, counts_ref, pooled_ref, got, send_sem, recv_sem):
    me = lax.axis_index("seq")
    right, left = lax.rem(me + 1, n), lax.rem(me + n - 1, n)
    greet(n, me)
    copies = [
        pltpu.make_async_remote_copy(
            src_ref=sides_ref.at[i], dst_ref=got.at[i], send_sem=send_sem.at[i], recv_sem=recv_sem.at[i],
            device_id={"seq": dev}, device_id_type=MESH)
        for i, dev in ((0, left), (1, right))
    ]
    for c in copies:
        c.start()
    cols = [jnp.transpose(jnp.broadcast_to(counts_ref[pl.ds(r, 1), :].astype(F32), (LANES, LANES)))
            for r in range(counts_ref.shape[0])]
    for c in copies:
        c.wait()
    for r, col in enumerate(cols):
        at = pl.ds(r * LANES, LANES)
        sums = own_ref[at, :] + got[0, at, :].astype(F32) + got[1, at, :].astype(F32)
        pooled_ref[at, :] = (sums / col).astype(BF16)


VM = pl.BlockSpec(memory_space=pltpu.VMEM)
ANY = pl.BlockSpec(memory_space=pl.ANY)
SM = pl.BlockSpec(memory_space=pltpu.SMEM)


def shards(n, token_cond, atom_feat, atom_counts, w_token, w_query, w_key, w_value, w_out, w_back):
    tok, _ = token_cond.shape
    atom_rows, width = atom_feat.shape
    crow = tok // LANES
    counts = atom_counts.reshape(crow, LANES)
    nrow = 3 * crow + 4
    trows = 3 * tok + 3 * LANES
    S = jax.ShapeDtypeStruct
    DMA = pltpu.SemaphoreType.DMA
    prows = -(-(8 + crow * n + nrow) // 8) * 8
    table, halo, ends, starts = pl.pallas_call(
        functools.partial(spread, n, atom_rows),
        name="spread",
        out_shape=(S((trows, width), BF16), S((2 * HALO, width), BF16),
                   S((nrow, LANES), jnp.int32), S((nrow, LANES), jnp.int32)),
        in_specs=[VM, VM, ANY, VM],
        out_specs=(ANY, ANY, VM, VM),
        scratch_shapes=[
            pltpu.VMEM((tok, width), BF16), pltpu.VMEM((LANES, width), BF16),
            pltpu.VMEM((n - 1, crow, LANES), jnp.int32), pltpu.VMEM((prows, LANES), jnp.int32),
            pltpu.VMEM((prows, LANES), jnp.int32),
            DMA((6,)), DMA((6,)), DMA((n - 1,)), DMA((n - 1,)), DMA((2,)),
        ],
        compiler_params=pltpu.CompilerParams(collective_id=0, has_side_effects=True),
    )(token_cond, w_token, atom_feat, counts)
    wqkv = jnp.concatenate([w_query, w_key, w_value], axis=1)
    atom_out, own, sides = pl.pallas_call(
        functools.partial(atoms, n),
        name="atoms",
        out_shape=(S((atom_rows, width), BF16), S((tok, width), F32), S((2, tok, width), BF16)),
        in_specs=[SM, VM, VM, VM, VM, VM, VM, VM],
        out_specs=(VM, VM, VM),
        scratch_shapes=[
            pltpu.VMEM((atom_rows, width), BF16), pltpu.VMEM((atom_rows, width), BF16),
            pltpu.VMEM((atom_rows + 2 * HALO, width), BF16), pltpu.VMEM((atom_rows + 2 * HALO, width), BF16),
            pltpu.VMEM((atom_rows, 2 * LANES), BF16), pltpu.VMEM((trows, width), F32),
        ],
    )(ends, table, halo, atom_feat, ends, starts, wqkv, w_out)
    pooled = pl.pallas_call(
        functools.partial(merge, n),
        name="merge",
        out_shape=S((tok, width), BF16),
        in_specs=[VM, VM, VM],
        out_specs=VM,
        scratch_shapes=[pltpu.VMEM((2, tok, width), BF16), DMA((2,)), DMA((2,))],
        compiler_params=pltpu.CompilerParams(collective_id=1, has_side_effects=True),
    )(own, sides, counts)
    token_out = (
        token_cond.astype(F32) + jnp.dot(pooled, w_back, preferred_element_type=F32)
    ).astype(BF16)
    return (token_out, atom_out)


def solution(mesh):
    both = P(("batch", "seq"), None)
    in_specs = (both, both, P(("batch", "seq")), P(), P(), P(), P(), P(), P())
    return jax.shard_map(
        functools.partial(shards, mesh.shape["seq"]), mesh=mesh, in_specs=in_specs, out_specs=(both, both),
        check_vma=False)
```

profile of v0, /device:TPU:0, one launch (start us, length us, event | category | flops | bytes accessed | tf_op | source)
XLA Modules:
  0.0 51.9 jit_solution(17266434201045683737)
XLA Ops:
  0.6 0.0 copy-start
  0.6 1.5 %pad_maximum_fusion.wqkv = bf16[128,384]{1,0:T(8,128)(2,1)} fusion(bf16[128,128]{1,0:T(8,128)(2,1)} %param.15, bf16[128,128]{1,0:T(8,128)(2,1)} %param.14, bf16[128,128]{1,0:T(8,128)(2,1)} %param.13), kind=kLoop, calls=%fused_computation.1 | loop fusion | flops 294912 | bytes 196608 | tf_op jit(solution)/shard_map/concatenate | solution.py:257
  2.1 13.4 %spread.1 = (bf16[1920,128]{1,0:T(8,128)(2,1)}, bf16[96,128]{1,0:T(8,128)(2,1)}, s32[16,128]{1,0:T(8,128)}, s32[16,128]{1,0:T(8,128)}) custom-call(bf16[512,768]{1,0:T(8,128)(2,1)} %cond_ref.1, bf16[768,128]{1,0:T(8,128)(2,1)} %wtok_ref.1, bf16[4096,128]{1,0:T(8,128)(2,1)} %feat.1, s32[4,128]{1,0:T(4,128)} %bitcast.3), custom_call_target="tpu_custom_call" | custom-call | tf_op jit(solution)/shard_map/spread/pallas_call | solution.py:242
  15.6 0.0 copy-start.1
  15.6 24.3 %atoms.1 = (bf16[4096,128]{1,0:T(8,128)(2,1)}, f32[512,128]{1,0:T(8,128)}, bf16[2,512,128]{2,1,0:T(8,128)(2,1)}) custom-call(s32[16,128]{1,0:T(8,128)} %get-tuple-element.9.ends_s.ends_v, bf16[1920,128]{1,0:T(8,128)(2,1)} %get-tuple-element.10.table, bf16[96,128]{1,0:T(8,128)(2,1)} %get-tuple-element.11.halo, bf16[4096,128]{1,0:T(8,128)(2,1)} %feat.1, ...), custom_call_target="tpu_custom_call" | custom-call | tf_op jit(solution)/shard_map/atoms/pallas_call | solution.py:258
  39.8 9.9 %merge.1 = bf16[512,128]{1,0:T(8,128)(2,1)} custom-call(f32[512,128]{1,0:T(8,128)} %get-tuple-element.13.own_ref, bf16[2,512,128]{2,1,0:T(8,128)(2,1)} %get-tuple-element.14.sides_ref, s32[4,128]{1,0:T(4,128)} %bitcast.4), custom_call_target="tpu_custom_call" | custom-call | tf_op jit(solution)/shard_map/merge/pallas_call | solution.py:270
  49.8 0.0 copy-done
  49.8 0.0 copy-done.1
  49.8 2.1 %add_convert_fusion = bf16[512,768]{1,0:T(8,128)(2,1)} fusion(bf16[512,768]{1,0:T(8,128)(2,1)S(1)} %copy-done.1, bf16[512,128]{1,0:T(8,128)(2,1)} %merge.1, bf16[128,768]{1,0:T(8,128)(2,1)S(1)} %copy-done), kind=kOutput, calls=%fused_computation | convolution fusion | flops 101842944 | bytes 1900544 | tf_op jit(solution)/shard_map/dot_general | solution.py:280
Async XLA Ops:
  0.6 49.1 %copy-start = (bf16[128,768]{1,0:T(8,128)(2,1)S(1)}, bf16[128,768]{1,0:T(8,128)(2,1)}, u32[]{:S(2)}) copy-start(bf16[128,768]{1,0:T(8,128)(2,1)} %param.17) | copy-start | bytes 589828
  15.6 34.2 %copy-start.1 = (bf16[512,768]{1,0:T(8,128)(2,1)S(1)}, bf16[512,768]{1,0:T(8,128)(2,1)}, u32[]{:S(2)}) copy-start(bf16[512,768]{1,0:T(8,128)(2,1)} %cond_ref.1) | copy-start | bytes 2359300
where the time goes:
time: 52.1 us; the launch traced here: 51.9 us
  Pallas kernels  47.6 us (91%)
  matrix products  2.13 us (4%)
  other arithmetic  1.48 us (3%)
  between operations  0.68 us (1%)
    pallas_call x1, Pallas kernels, shards(): pl.pallas_call(functools.partial(atoms, n), name='atoms', out_shape=(S((a...  24.3 us
    pallas_call x1, Pallas kernels, shards(): pl.pallas_call(functools.partial(spread, n, atom_rows), name='spread', ou...  13.4 us
    pallas_call x1, Pallas kernels, shards(): pl.pallas_call(functools.partial(merge, n), name='merge', out_shape=S((to...  9.9 us
    dot_general x1, matrix products, shards(): jnp.dot(pooled, w_back, preferred_element_type=F32)  2.13 us
    concatenate x1, other arithmetic, shards(): wqkv = jnp.concatenate([w_query, w_key, w_value], axis=1)  1.48 us

commit v1 on v0

v1 whole, which is shorter than its diff:
```python
import functools
import math

import jax
import jax.numpy as jnp
from jax import lax
from jax.experimental import pallas as pl
from jax.experimental.pallas import tpu as pltpu
from jax.sharding import PartitionSpec as P

HEADS = 4
QBLOCK = 32
KEYS = 128
HALO = 48
LANES = 128
MESH = pl.DeviceIdType.MESH
F32 = jnp.float32
BF16 = jnp.bfloat16


def dot(a, b, dims=((1,), (0,))):
    return lax.dot_general(a, b, (dims, ((), ())), preferred_element_type=F32)


def greet(n, me):
    barrier = pltpu.get_barrier_semaphore()
    for d in range(1, n):
        pl.semaphore_signal(barrier, inc=1, device_id={"seq": lax.rem(me + d, n)}, device_id_type=MESH)
    return lambda: pl.semaphore_wait(barrier, n - 1)


def spread(n, atom_rows, cond_ref, wtok_ref, feat_ref, counts_ref, table_ref, halo_ref, ends_ref, starts_ref, wins_ref,
           proj, zeros, cnt, padded, ends_all, send_sem, recv_sem, csend, crecv, lsem):
    me = lax.axis_index("seq")
    tok = cond_ref.shape[0]
    crow = tok // LANES
    right, left = lax.rem(me + 1, n), lax.rem(me + n - 1, n)
    right2, left2 = lax.rem(me + 2, n), lax.rem(me + n - 2, n)

    def remote(i, src, dst, dev):
        return pltpu.make_async_remote_copy(
            src_ref=src, dst_ref=dst, send_sem=send_sem.at[i], recv_sem=recv_sem.at[i],
            device_id={"seq": dev}, device_id_type=MESH)

    arrive = greet(n, me)
    half = tok // 2
    proj[pl.ds(0, half), :] = dot(cond_ref[pl.ds(0, half), :], wtok_ref[...]).astype(BF16)
    arrive()
    ccopies = []
    for d in range(1, n):
        c = pltpu.make_async_remote_copy(
            src_ref=counts_ref, dst_ref=cnt.at[d - 1], send_sem=csend.at[d - 1], recv_sem=crecv.at[d - 1],
            device_id={"seq": lax.rem(me + d, n)}, device_id_type=MESH)
        c.start()
        ccopies.append(c)

    def pair(i, at):
        return [
            remote(i, proj.at[pl.ds(at, half)], table_ref.at[pl.ds(LANES + at, half)], right),
            remote(i + 1, proj.at[pl.ds(at, half)], table_ref.at[pl.ds(LANES + 2 * tok + at, half)], left),
        ]

    copies = pair(0, 0)
    for c in copies:
        c.start()
    proj[pl.ds(half, half), :] = dot(cond_ref[pl.ds(half, half), :], wtok_ref[...]).astype(BF16)
    more = pair(2, half) + [
        remote(4, proj.at[pl.ds(tok - LANES, LANES)], table_ref.at[pl.ds(0, LANES)], right2),
        remote(5, proj.at[pl.ds(0, LANES)], table_ref.at[pl.ds(LANES + 3 * tok, LANES)], left2),
        remote(6, feat_ref.at[pl.ds(atom_rows - HALO, HALO)], halo_ref.at[pl.ds(0, HALO)], right),
        remote(7, feat_ref.at[pl.ds(0, HALO)], halo_ref.at[pl.ds(HALO, HALO)], left),
    ]
    for c in more:
        c.start()
    zeros[...] = jnp.zeros_like(zeros)
    own = pltpu.make_async_copy(proj, table_ref.at[pl.ds(LANES + tok, tok)], lsem.at[0])
    own.start()
    tail = pltpu.make_async_copy(zeros, table_ref.at[pl.ds(2 * LANES + 3 * tok, LANES)], lsem.at[1])
    tail.start()

    padded[...] = jnp.zeros_like(padded)
    rows = padded.shape[0]
    for c in ccopies:
        c.wait()
    for j in range(n):
        part = jnp.where(me == j, counts_ref[...], 0)
        for d in range(1, n):
            part = jnp.where(lax.rem(me + n - d, n) == j, cnt[d - 1], part)
        padded[pl.ds(8 + crow * j, crow), :] = part
    counts = padded[...].astype(F32).astype(BF16)
    tri = (lax.broadcasted_iota(jnp.int32, (LANES, LANES), 0)
           <= lax.broadcasted_iota(jnp.int32, (LANES, LANES), 1)).astype(F32).astype(BF16)
    before = (lax.broadcasted_iota(jnp.int32, (rows, rows), 1)
              < lax.broadcasted_iota(jnp.int32, (rows, rows), 0)).astype(F32).astype(BF16)
    inner = dot(counts, tri)
    outer = jnp.sum(dot(before, counts), axis=1, keepdims=True)
    ends_all[...] = (inner + outer).astype(jnp.int32)
    near = pl.ds(8 - 1 - crow + crow * me, ends_ref.shape[0])
    ends = ends_all[near, :] - me * atom_rows
    ends_ref[...] = ends
    starts_ref[...] = ends - padded[near, :]
    first = jnp.where(lax.broadcasted_iota(jnp.int32, wins_ref.shape, 0) == 0,
                      lax.broadcasted_iota(jnp.int32, wins_ref.shape, 1) * LANES, -HALO)
    w = jnp.zeros_like(first)
    for r in range(ends_ref.shape[0] - 1):
        w += jnp.where(ends[r:r + 1, LANES - 1:] <= first, 1, 0)
    wins_ref[...] = jnp.minimum(w, ends_ref.shape[0] - 3)
    for c in copies + more:
        c.wait()
    own.wait()
    tail.wait()


def atoms(n, group, wins, table, halo, feat, ends_v, starts_v, wq, wk, wv, wout, out, own, sides,
          obuf, wqkv, xs, qs, ks, vs, att, mem, pool, osem):
    me = lax.axis_index("seq")
    atom_rows, width = feat.shape
    tok = own.shape[0]
    head = width // HEADS
    nrow = ends_v.shape[0]
    scale = math.log2(math.e) / math.sqrt(head)
    step = group * LANES
    tiles = atom_rows // LANES
    groups = atom_rows // step
    spare = pool.shape[0] - 2 * LANES

    def store(g):
        at = pl.ds(pl.multiple_of(g * step, step), step)
        return pltpu.make_async_copy(obuf.at[at], out.at[at], osem.at[g])

    def each(f):
        def body(g, c):
            f(g)
            return c
        return body

    for i, w in enumerate((wq, wk, wv)):
        wqkv[:, i * width:(i + 1) * width] = w[...]

    def gather(w, first, f):
        r = f.shape[0]
        ids = first + lax.broadcasted_iota(jnp.int32, (r, LANES), 0)
        parts = []
        for s in range(2):
            lo = starts_v[pl.ds(w + s, 1), :]
            hi = ends_v[pl.ds(w + s, 1), :]
            parts.append(jnp.where((ids >= lo) & (ids < hi), F32(1), F32(0)).astype(BF16))
        member = jnp.concatenate(parts, axis=1)
        rows = dot(member, table[pl.ds(pl.multiple_of(w * LANES, LANES), 2 * LANES), :])
        x = (f.astype(F32) + rows).astype(BF16)
        return member, x

    def keyval(at, qkv, r):
        ks[pl.ds(at, r), :] = qkv[:, width:2 * width].astype(BF16)
        vs[pl.ds(at, r), :] = qkv[:, 2 * width:].astype(BF16)

    for first, at in ((-HALO, 0), (atom_rows, atom_rows + HALO)):
        f = halo[pl.ds(0 if first < 0 else HALO, HALO), :]
        w = wins[1, 0] if first < 0 else wins[0, tiles]
        _, x = gather(w, jnp.int32(first), f)
        keyval(at, dot(x, wqkv[...]), HALO)
    pool[...] = jnp.zeros_like(pool)

    lane = lax.broadcasted_iota(jnp.int32, (1, width), 1)
    hmask = [((lane >= h * head) & (lane < (h + 1) * head)) for h in range(HEADS)]
    hmul = [jnp.where(m, F32(1), F32(0)).astype(BF16) for m in hmask]
    ones = jnp.ones((KEYS, width), BF16)
    total = atom_rows * n
    klane = lax.broadcasted_iota(jnp.int32, (1, KEYS), 1)
    per = LANES // QBLOCK

    def pick(o):
        r = o[(HEADS - 1) * QBLOCK:]
        for h in range(HEADS - 2, -1, -1):
            r = jnp.where(hmask[h], o[h * QBLOCK:(h + 1) * QBLOCK], r)
        return r

    def gathers(g):
        made = []
        for u in range(group):
            a = pl.multiple_of(g * step + u * LANES, LANES)
            made.append((a, *gather(wins[0, g * group + u], a, feat[pl.ds(a, LANES), :])))
        return made

    def project(g, made):
        qkvs = [dot(x, wqkv[...]) for _, _, x in made]
        for (a, member, x), qkv in zip(made, qkvs):
            mem[pl.ds(a, LANES), :] = member
            xs[pl.ds(a, LANES), :] = x
            qs[pl.ds(a, LANES), :] = qkv[:, :width].astype(BF16)
            keyval(pl.multiple_of(a + HALO, 16), qkv, LANES)

    def scored(g, js):
        scores = []
        for j in js:
            at = pl.multiple_of(g * step + j * QBLOCK, QBLOCK)
            q = qs[pl.ds(at, QBLOCK), :]
            qb = jnp.concatenate([q * m for m in hmul], axis=0)
            s = dot(qb, ks[pl.ds(at, KEYS), :], ((1,), (1,)))
            pos = me * atom_rows + at - HALO + klane
            scores.append(jnp.where((pos >= 0) & (pos < total), s, F32(-1e30)))
        return scores

    def soft(scores):
        probs = []
        for s in scores:
            m = jnp.max(s, axis=1, keepdims=True)
            probs.append(jnp.exp2((s - m) * F32(scale)).astype(BF16))
        return probs

    def attend(g, js, probs):
        raw = []
        for j, p in zip(js, probs):
            at = pl.multiple_of(g * step + j * QBLOCK, QBLOCK)
            raw.append(dot(p, jnp.concatenate([vs[pl.ds(at, KEYS), :], ones], axis=1)))
        return [(pick(o[:, :width]) / pick(o[:, width:])).astype(BF16) for o in raw]

    def residual(g):
        at = pl.ds(pl.multiple_of(g * step, step), step)
        y = (xs[at, :].astype(F32) + dot(att[at, :], wout[...])).astype(BF16)
        obuf[at, :] = y
        return y

    def pooled(g, y, real):
        parts = [dot(mem[pl.ds(pl.multiple_of(g * step + u * LANES, LANES), LANES), :],
                     y[u * LANES:(u + 1) * LANES], ((0,), (0,))) for u in range(group)]
        for u, part in enumerate(parts):
            first = jnp.where(real, wins[0, g * group + u] * LANES, spare)
            pool[pl.ds(pl.multiple_of(first, LANES), 2 * LANES), :] += part

    early, late = range(group * per // 2), range(group * per // 2, group * per)
    ahead = 2

    def advance(g, more):
        past = jnp.maximum(g - 1, 0)
        s0 = scored(g, early)
        y = residual(past)
        made = gathers(g + ahead) if more else None
        p0 = soft(s0)
        s1 = scored(g, late)
        pooled(past, y, g > 0)
        o0 = attend(g, early, p0)
        p1 = soft(s1)
        o1 = attend(g, late, p1)
        if more:
            project(g + ahead, made)
        att[pl.ds(pl.multiple_of(g * step, step), step), :] = jnp.concatenate(o0 + o1, axis=0)

        @pl.when(g > 0)
        def _():
            store(past).start()

    lax.fori_loop(0, ahead, each(lambda g: project(g, gathers(g))), 0)
    lax.fori_loop(0, groups - ahead, each(lambda g: advance(g, True)), 0)
    lax.fori_loop(groups - ahead, groups, each(lambda g: advance(g, False)), 0)
    y = residual(groups - 1)
    store(groups - 1).start()
    pooled(groups - 1, y, True)
    own[...] = pool[pl.ds(LANES + tok, tok), :]
    sides[0] = pool[pl.ds(LANES, tok), :].astype(BF16)
    sides[1] = pool[pl.ds(LANES + 2 * tok, tok), :].astype(BF16)
    lax.fori_loop(0, groups, each(lambda g: store(g).wait()), 0)


def merge(n, own_ref, sides_ref, counts_ref, pooled_ref, got, send_sem, recv_sem):
    me = lax.axis_index("seq")
    right, left = lax.rem(me + 1, n), lax.rem(me + n - 1, n)
    greet(n, me)()
    copies = [
        pltpu.make_async_remote_copy(
            src_ref=sides_ref.at[i], dst_ref=got.at[i], send_sem=send_sem.at[i], recv_sem=recv_sem.at[i],
            device_id={"seq": dev}, device_id_type=MESH)
        for i, dev in ((0, left), (1, right))
    ]
    for c in copies:
        c.start()
    cols = [jnp.transpose(jnp.broadcast_to(counts_ref[pl.ds(r, 1), :].astype(F32), (LANES, LANES)))
            for r in range(counts_ref.shape[0])]
    for c in copies:
        c.wait()
    for r, col in enumerate(cols):
        at = pl.ds(r * LANES, LANES)
        sums = own_ref[at, :] + got[0, at, :].astype(F32) + got[1, at, :].astype(F32)
        pooled_ref[at, :] = (sums / col).astype(BF16)


VM = pl.BlockSpec(memory_space=pltpu.VMEM)
ANY = pl.BlockSpec(memory_space=pl.ANY)
HBM = pl.BlockSpec(memory_space=pltpu.HBM)
SM = pl.BlockSpec(memory_space=pltpu.SMEM)


def shards(n, token_cond, atom_feat, atom_counts, w_token, w_query, w_key, w_value, w_out, w_back):
    tok, _ = token_cond.shape
    atom_rows, width = atom_feat.shape
    crow = tok // LANES
    counts = atom_counts.reshape(crow, LANES)
    nrow = 3 * crow + 4
    trows = 3 * tok + 3 * LANES
    S = jax.ShapeDtypeStruct
    DMA = pltpu.SemaphoreType.DMA
    prows = -(-(8 + crow * n + nrow) // 8) * 8
    table, halo, ends, starts, wins = pl.pallas_call(
        functools.partial(spread, n, atom_rows),
        name="spread",
        out_shape=(S((trows, width), BF16), S((2 * HALO, width), BF16),
                   S((nrow, LANES), jnp.int32), S((nrow, LANES), jnp.int32),
                   S((8, LANES), jnp.int32)),
        in_specs=[VM, VM, HBM, VM],
        out_specs=(ANY, ANY, VM, VM, VM),
        scratch_shapes=[
            pltpu.VMEM((tok, width), BF16), pltpu.VMEM((LANES, width), BF16),
            pltpu.VMEM((n - 1, crow, LANES), jnp.int32), pltpu.VMEM((prows, LANES), jnp.int32),
            pltpu.VMEM((prows, LANES), jnp.int32),
            DMA((8,)), DMA((8,)), DMA((n - 1,)), DMA((n - 1,)), DMA((2,)),
        ],
        compiler_params=pltpu.CompilerParams(collective_id=0, has_side_effects=True, vmem_limit_bytes=8 << 20),
    )(token_cond, w_token, atom_feat, counts)
    group = 2
    groups = atom_rows // (group * LANES)
    atom_out, own, sides = pl.pallas_call(
        functools.partial(atoms, n, group),
        name="atoms",
        out_shape=(S((atom_rows, width), BF16), S((tok, width), F32), S((2, tok, width), BF16)),
        in_specs=[SM, VM, VM, VM, VM, VM, VM, VM, VM, VM],
        out_specs=(ANY, VM, VM),
        scratch_shapes=[
            pltpu.VMEM((atom_rows, width), BF16), pltpu.VMEM((width, 3 * width), BF16),
            pltpu.VMEM((atom_rows, width), BF16), pltpu.VMEM((atom_rows, width), BF16),
            pltpu.VMEM((atom_rows + 2 * HALO, width), BF16), pltpu.VMEM((atom_rows + 2 * HALO, width), BF16),
            pltpu.VMEM((atom_rows, width), BF16), pltpu.VMEM((atom_rows, 2 * LANES), BF16),
            pltpu.VMEM((trows + 2 * LANES, width), F32),
            DMA((groups,)),
        ],
        compiler_params=pltpu.CompilerParams(vmem_limit_bytes=24 << 20),
    )(wins, table, halo, atom_feat, ends, starts, w_query, w_key, w_value, w_out)
    pooled = pl.pallas_call(
        functools.partial(merge, n),
        name="merge",
        out_shape=S((tok, width), BF16),
        in_specs=[VM, VM, VM],
        out_specs=VM,
        scratch_shapes=[pltpu.VMEM((2, tok, width), BF16), DMA((2,)), DMA((2,))],
        compiler_params=pltpu.CompilerParams(collective_id=1, has_side_effects=True, vmem_limit_bytes=8 << 20),
    )(own, sides, counts)
    token_out = (
        token_cond.astype(F32) + jnp.dot(pooled, w_back, preferred_element_type=F32)
    ).astype(BF16)
    return (token_out, atom_out)


def solution(mesh):
    both = P(("batch", "seq"), None)
    in_specs = (both, both, P(("batch", "seq")), P(), P(), P(), P(), P(), P())
    return jax.shard_map(
        functools.partial(shards, mesh.shape["seq"]), mesh=mesh, in_specs=in_specs, out_specs=(both, both),
        check_vma=False)
```

time: 52.1 us -> 38.6 us (0.74)
  Pallas kernels: 47.6 us -> 32.3 us
  local copies, waits for them, and re-layouts: 0.02 us -> 4.04 us
  other arithmetic: 1.48 us -> 0 us
  matrix products: 2.13 us -> 1.23 us
    pallas_call x1, Pallas kernels: 24.3 us -> 12.7 us  [shards(): pl.pallas_call(functools.partial(atoms, n, group), name='atoms', out_shap...]
    unnamed x4 -> x24, local copies, waits for them, and re-layouts: 0.02 us -> 4.04 us
    pallas_call x1, Pallas kernels: 13.4 us -> 11.4 us  [shards(): pl.pallas_call(functools.partial(spread, n, atom_rows), name='spread', ou...]
    pallas_call x1, Pallas kernels: 9.9 us -> 8.25 us  [shards(): pl.pallas_call(functools.partial(merge, n), name='merge', out_shape=S((to...]
    concatenate x1 -> x0, other arithmetic: 1.48 us -> none  [shards(): wqkv = jnp.concatenate([w_query, w_key, w_value], axis=1)]
    dot_general x1, matrix products: 2.13 us -> 1.23 us  [shards(): jnp.dot(pooled, w_back, preferred_element_type=F32)]
where the time goes in v1:
time: 38.6 us; the launch traced here: 38.4 us
  Pallas kernels  32.3 us (84%)
  local copies, waits for them, and re-layouts  4.04 us (10%)
  matrix products  1.23 us (3%)
  between operations  0.77 us (2%)
    pallas_call x1, Pallas kernels, shards(): pl.pallas_call(functools.partial(atoms, n, group), name='atoms', out_shap...  12.7 us
    pallas_call x1, Pallas kernels, shards(): pl.pallas_call(functools.partial(spread, n, atom_rows), name='spread', ou...  11.4 us
    pallas_call x1, Pallas kernels, shards(): pl.pallas_call(functools.partial(merge, n), name='merge', out_shape=S((to...  8.25 us
    unnamed x24, local copies, waits for them, and re-layouts  4.04 us
    dot_general x1, matrix products, shards(): jnp.dot(pooled, w_back, preferred_element_type=F32)  1.23 us

profile of v1, /device:TPU:0, one launch (start us, length us, event | category | flops | bytes accessed | tf_op | source)
XLA Modules:
  0.0 38.4 jit_solution(2583165815584819466)
XLA Ops:
  0.6 0.0 copy-start
  0.6 0.0 copy-start.1
  0.7 1.3 %copy-done.1 = bf16[4096,128]{1,0:T(8,128)(2,1)S(1)} copy-done((bf16[4096,128]{1,0:T(8,128)(2,1)S(1)}, bf16[4096,128]{1,0:T(8,128)(2,1)}, u32[]{:S(2)}) %copy-start.1) | copy-done | bytes 1048600
  1.9 0.0 copy-start.3
  1.9 1.1 %copy-done.3 = bf16[512,768]{1,0:T(8,128)(2,1)S(1)} copy-done((bf16[512,768]{1,0:T(8,128)(2,1)S(1)}, bf16[512,768]{1,0:T(8,128)(2,1)}, u32[]{:S(2)}) %copy-start.3) | copy-done | bytes 786456
  3.0 0.0 copy-start.5
  3.0 0.9 %copy-done.5 = bf16[768,128]{1,0:T(8,128)(2,1)S(1)} copy-done((bf16[768,128]{1,0:T(8,128)(2,1)S(1)}, bf16[768,128]{1,0:T(8,128)(2,1)}, u32[]{:S(2)}) %copy-start.5) | copy-done | bytes 196632
  4.0 0.0 copy-start.10
  4.0 0.7 %copy-done.10 = s32[512]{0:T(512)S(1)} copy-done((s32[512]{0:T(512)S(1)}, s32[512]{0:T(512)}, u32[]{:S(2)}) %copy-start.10) | copy-done | bytes 2072
  4.7 0.0 copy-start.2
  4.7 0.0 copy-start.6
  4.7 0.0 copy-start.7
  4.7 0.0 copy-start.8
  4.7 0.0 copy-start.9
  4.7 11.4 %spread.1 = (bf16[1920,128]{1,0:T(8,128)(2,1)S(1)}, bf16[96,128]{1,0:T(8,128)(2,1)S(1)}, s32[16,128]{1,0:T(8,128)S(1)}, s32[16,128]{1,0:T(8,128)S(1)}, s32[8,128]{1,0:T(8,128)S(1)}) custom-call(bf16[512,768]{1,0:T(8,128)(2,1)S(1)} %copy-done.3, bf16[768,128]{1,0:T(8,128)(2,1)S(1)} %copy-done.5, bf16[4096,128]{1,0:T(8,128)(2,1)S(1)} %copy-done.1, ...), custom_call_target="tpu_custom_call" | custom-call | tf_op jit(solution)/shard_map/spread/pallas_call | solution.py:303
  16.1 0.0 copy-start.11
  16.1 0.0 copy-done.2
  16.1 0.0 copy-done.6
  16.1 0.0 copy-done.7
  16.1 0.0 copy-done.8
  16.1 0.0 copy-done.9
  16.1 0.0 copy-start.4
  16.1 12.7 %atoms.1 = (bf16[4096,128]{1,0:T(8,128)(2,1)}, f32[512,128]{1,0:T(8,128)S(1)}, bf16[2,512,128]{2,1,0:T(8,128)(2,1)S(1)}) custom-call(s32[8,128]{1,0:T(8,128)S(1)} %get-tuple-element.10.wins, bf16[1920,128]{1,0:T(8,128)(2,1)S(1)} %get-tuple-element.11.table, bf16[96,128]{1,0:T(8,128)(2,1)S(1)} %get-tuple-element.12.halo, bf16[4096,128]{1,0:T(8,128)(2,1)S(1)} %copy-done.2, ...), custom_call_target="tpu_custom_call" | custom-call | tf_op jit(solution)/shard_map/atoms/pallas_call | solution.py:321
  28.8 0.0 copy-done.11
  28.9 8.2 %merge.1 = bf16[512,128]{1,0:T(8,128)(2,1)S(1)} custom-call(f32[512,128]{1,0:T(8,128)S(1)} %get-tuple-element.15.own_ref, bf16[2,512,128]{2,1,0:T(8,128)(2,1)S(1)} %get-tuple-element.16.sides_ref, s32[4,128]{1,0:T(4,128)S(1)} %bitcast.4), custom_call_target="tpu_custom_call" | custom-call | tf_op jit(solution)/shard_map/merge/pallas_call | solution.py:337
  37.1 0.0 copy-done
  37.1 0.0 copy-done.4
  37.1 1.2 %add_convert_fusion = bf16[512,768]{1,0:T(8,128)(2,1)} fusion(bf16[512,768]{1,0:T(8,128)(2,1)S(1)} %copy-done.4, bf16[512,128]{1,0:T(8,128)(2,1)S(1)} %merge.1, bf16[128,768]{1,0:T(8,128)(2,1)S(1)} %copy-done), kind=kOutput, calls=%fused_computation | convolution fusion | flops 101842944 | bytes 1900544 | tf_op jit(solution)/shard_map/dot_general | solution.py:347
Async XLA Ops:
  0.6 36.5 %copy-start = (bf16[128,768]{1,0:T(8,128)(2,1)S(1)}, bf16[128,768]{1,0:T(8,128)(2,1)}, u32[]{:S(2)}) copy-start(bf16[128,768]{1,0:T(8,128)(2,1)} %param.17) | copy-start | bytes 589828
  0.6 1.3 %copy-start.1 = (bf16[4096,128]{1,0:T(8,128)(2,1)S(1)}, bf16[4096,128]{1,0:T(8,128)(2,1)}, u32[]{:S(2)}) copy-start(bf16[4096,128]{1,0:T(8,128)(2,1)} %feat.1) | copy-start | bytes 3145732
  1.9 1.1 %copy-start.3 = (bf16[512,768]{1,0:T(8,128)(2,1)S(1)}, bf16[512,768]{1,0:T(8,128)(2,1)}, u32[]{:S(2)}) copy-start(bf16[512,768]{1,0:T(8,128)(2,1)} %cond_ref.1) | copy-start | bytes 2359300
  3.0 0.9 %copy-start.5 = (bf16[768,128]{1,0:T(8,128)(2,1)S(1)}, bf16[768,128]{1,0:T(8,128)(2,1)}, u32[]{:S(2)}) copy-start(bf16[768,128]{1,0:T(8,128)(2,1)} %wtok_ref.1) | copy-start | bytes 589828
  4.0 0.7 %copy-start.10 = (s32[512]{0:T(512)S(1)}, s32[512]{0:T(512)}, u32[]{:S(2)}) copy-start(s32[512]{0:T(512)} %param.11) | copy-start | bytes 6148
  4.7 11.4 %copy-start.2 = (bf16[4096,128]{1,0:T(8,128)(2,1)S(1)}, bf16[4096,128]{1,0:T(8,128)(2,1)}, u32[]{:S(2)}) copy-start(bf16[4096,128]{1,0:T(8,128)(2,1)} %feat.1) | copy-start | bytes 3145732
  4.7 11.4 %copy-start.6 = (bf16[128,128]{1,0:T(8,128)(2,1)S(1)}, bf16[128,128]{1,0:T(8,128)(2,1)}, u32[]{:S(2)}) copy-start(bf16[128,128]{1,0:T(8,128)(2,1)} %wq.1) | copy-start | bytes 98308
  4.7 11.4 %copy-start.7 = (bf16[128,128]{1,0:T(8,128)(2,1)S(1)}, bf16[128,128]{1,0:T(8,128)(2,1)}, u32[]{:S(2)}) copy-start(bf16[128,128]{1,0:T(8,128)(2,1)} %wk.1) | copy-start | bytes 98308
  4.7 11.5 %copy-start.8 = (bf16[128,128]{1,0:T(8,128)(2,1)S(1)}, bf16[128,128]{1,0:T(8,128)(2,1)}, u32[]{:S(2)}) copy-start(bf16[128,128]{1,0:T(8,128)(2,1)} %wv.1) | copy-start | bytes 98308
  4.7 11.5 %copy-start.9 = (bf16[128,128]{1,0:T(8,128)(2,1)S(1)}, bf16[128,128]{1,0:T(8,128)(2,1)}, u32[]{:S(2)}) copy-start(bf16[128,128]{1,0:T(8,128)(2,1)} %wout.1) | copy-start | bytes 98308
  16.1 12.8 %copy-start.11 = (s32[512]{0:T(512)S(1)}, s32[512]{0:T(512)}, u32[]{:S(2)}) copy-start(s32[512]{0:T(512)} %param.11) | copy-start | bytes 6148
  16.1 21.0 %copy-start.4 = (bf16[512,768]{1,0:T(8,128)(2,1)S(1)}, bf16[512,768]{1,0:T(8,128)(2,1)}, u32[]{:S(2)}) copy-start(bf16[512,768]{1,0:T(8,128)(2,1)} %cond_ref.1) | copy-start | bytes 2359300

commit v2 on v1

--- a/solution.py
+++ b/solution.py
@@ -29,8 +29,8 @@
     return lambda: pl.semaphore_wait(barrier, n - 1)
 
 
-def spread(n, atom_rows, cond_ref, wtok_ref, feat_ref, counts_ref, table_ref, halo_ref, ends_ref, starts_ref, wins_ref,
-           proj, zeros, cnt, padded, ends_all, send_sem, recv_sem, csend, crecv, lsem):
+def spread(n, atom_rows, cond_hbm, wtok_hbm, feat_ref, counts_ref, table_ref, halo_ref, ends_ref, starts_ref, wins_ref,
+           cond_ref, wtok_ref, proj, zeros, cnt, padded, ends_all, send_sem, recv_sem, csend, crecv, lsem):
     me = lax.axis_index("seq")
     tok = cond_ref.shape[0]
     crow = tok // LANES
@@ -42,8 +42,15 @@
             src_ref=src, dst_ref=dst, send_sem=send_sem.at[i], recv_sem=recv_sem.at[i],
             device_id={"seq": dev}, device_id_type=MESH)
 
+    half = tok // 2
+    loads = [pltpu.make_async_copy(wtok_hbm, wtok_ref, lsem.at[2])] + [
+        pltpu.make_async_copy(cond_hbm.at[pl.ds(i * half, half)], cond_ref.at[pl.ds(i * half, half)], lsem.at[3 + i])
+        for i in range(2)]
+    for c in loads:
+        c.start()
     arrive = greet(n, me)
-    half = tok // 2
+    loads[0].wait()
+    loads[1].wait()
     proj[pl.ds(0, half), :] = dot(cond_ref[pl.ds(0, half), :], wtok_ref[...]).astype(BF16)
     arrive()
     ccopies = []
@@ -63,6 +70,7 @@
     copies = pair(0, 0)
     for c in copies:
         c.start()
+    loads[2].wait()
     proj[pl.ds(half, half), :] = dot(cond_ref[pl.ds(half, half), :], wtok_ref[...]).astype(BF16)
     more = pair(2, half) + [
         remote(4, proj.at[pl.ds(tok - LANES, LANES)], table_ref.at[pl.ds(0, LANES)], right2),
@@ -111,8 +119,8 @@
     tail.wait()
 
 
-def atoms(n, group, wins, table, halo, feat, ends_v, starts_v, wq, wk, wv, wout, out, own, sides,
-          obuf, wqkv, xs, qs, ks, vs, att, mem, pool, osem):
+def atoms(n, group, wins, table, halo, feat_hbm, ends_v, starts_v, wq, wk, wv, wout, out, own, sides,
+          feat, obuf, wqkv, xs, qs, ks, vs, att, mem, pool, fsem, osem):
     me = lax.axis_index("seq")
     atom_rows, width = feat.shape
     tok = own.shape[0]
@@ -124,6 +132,10 @@
     groups = atom_rows // step
     spare = pool.shape[0] - 2 * LANES
 
+    def load(g):
+        at = pl.ds(pl.multiple_of(g * step, step), step)
+        return pltpu.make_async_copy(feat_hbm.at[at], feat.at[at], fsem.at[g])
+
     def store(g):
         at = pl.ds(pl.multiple_of(g * step, step), step)
         return pltpu.make_async_copy(obuf.at[at], out.at[at], osem.at[g])
@@ -134,6 +146,7 @@
             return c
         return body
 
+    lax.fori_loop(0, groups, each(lambda g: load(g).start()), 0)
     for i, w in enumerate((wq, wk, wv)):
         wqkv[:, i * width:(i + 1) * width] = w[...]
 
@@ -233,6 +246,8 @@
 
     def advance(g, more):
         past = jnp.maximum(g - 1, 0)
+        if more:
+            load(g + ahead).wait()
         s0 = scored(g, early)
         y = residual(past)
         made = gathers(g + ahead) if more else None
@@ -250,7 +265,11 @@
         def _():
             store(past).start()
 
-    lax.fori_loop(0, ahead, each(lambda g: project(g, gathers(g))), 0)
+    def begin(g):
+        load(g).wait()
+        project(g, gathers(g))
+
+    lax.fori_loop(0, ahead, each(begin), 0)
     lax.fori_loop(0, groups - ahead, each(lambda g: advance(g, True)), 0)
     lax.fori_loop(groups - ahead, groups, each(lambda g: advance(g, False)), 0)
     y = residual(groups - 1)
@@ -306,15 +325,16 @@
         out_shape=(S((trows, width), BF16), S((2 * HALO, width), BF16),
                    S((nrow, LANES), jnp.int32), S((nrow, LANES), jnp.int32),
                    S((8, LANES), jnp.int32)),
-        in_specs=[VM, VM, HBM, VM],
+        in_specs=[HBM, HBM, HBM, VM],
         out_specs=(ANY, ANY, VM, VM, VM),
         scratch_shapes=[
+            pltpu.VMEM(token_cond.shape, BF16), pltpu.VMEM(w_token.shape, BF16),
             pltpu.VMEM((tok, width), BF16), pltpu.VMEM((LANES, width), BF16),
             pltpu.VMEM((n - 1, crow, LANES), jnp.int32), pltpu.VMEM((prows, LANES), jnp.int32),
             pltpu.VMEM((prows, LANES), jnp.int32),
-            DMA((8,)), DMA((8,)), DMA((n - 1,)), DMA((n - 1,)), DMA((2,)),
+            DMA((8,)), DMA((8,)), DMA((n - 1,)), DMA((n - 1,)), DMA((5,)),
         ],
-        compiler_params=pltpu.CompilerParams(collective_id=0, has_side_effects=True, vmem_limit_bytes=8 << 20),
+        compiler_params=pltpu.CompilerParams(collective_id=0, has_side_effects=True, vmem_limit_bytes=62 << 20),
     )(token_cond, w_token, atom_feat, counts)
     group = 2
     groups = atom_rows // (group * LANES)
@@ -322,17 +342,18 @@
         functools.partial(atoms, n, group),
         name="atoms",
         out_shape=(S((atom_rows, width), BF16), S((tok, width), F32), S((2, tok, width), BF16)),
-        in_specs=[SM, VM, VM, VM, VM, VM, VM, VM, VM, VM],
+        in_specs=[SM, VM, VM, HBM, VM, VM, VM, VM, VM, VM],
         out_specs=(ANY, VM, VM),
         scratch_shapes=[
+            pltpu.VMEM((atom_rows, width), BF16),
             pltpu.VMEM((atom_rows, width), BF16), pltpu.VMEM((width, 3 * width), BF16),
             pltpu.VMEM((atom_rows, width), BF16), pltpu.VMEM((atom_rows, width), BF16),
             pltpu.VMEM((atom_rows + 2 * HALO, width), BF16), pltpu.VMEM((atom_rows + 2 * HALO, width), BF16),
             pltpu.VMEM((atom_rows, width), BF16), pltpu.VMEM((atom_rows, 2 * LANES), BF16),
             pltpu.VMEM((trows + 2 * LANES, width), F32),
-            DMA((groups,)),
+            DMA((groups,)), DMA((groups,)),
         ],
-        compiler_params=pltpu.CompilerParams(vmem_limit_bytes=24 << 20),
+        compiler_params=pltpu.CompilerParams(vmem_limit_bytes=62 << 20),
     )(wins, table, halo, atom_feat, ends, starts, w_query, w_key, w_value, w_out)
     pooled = pl.pallas_call(
         functools.partial(merge, n),
@@ -341,7 +362,7 @@
         in_specs=[VM, VM, VM],
         out_specs=VM,
         scratch_shapes=[pltpu.VMEM((2, tok, width), BF16), DMA((2,)), DMA((2,))],
-        compiler_params=pltpu.CompilerParams(collective_id=1, has_side_effects=True, vmem_limit_bytes=8 << 20),
+        compiler_params=pltpu.CompilerParams(collective_id=1, has_side_effects=True, vmem_limit_bytes=62 << 20),
     )(own, sides, counts)
     token_out = (
         token_cond.astype(F32) + jnp.dot(pooled, w_back, preferred_element_type=F32)

time: 38.6 us -> 41.6 us (1.078)
  Pallas kernels: 32.3 us -> 38.5 us
  local copies, waits for them, and re-layouts: 4.04 us -> 0.02 us
  matrix products: 1.23 us -> 2.13 us
    unnamed x24 -> x4, local copies, waits for them, and re-layouts: 4.04 us -> 0.02 us
    pallas_call x1, Pallas kernels: 11.4 us -> 13.8 us  [shards(): pl.pallas_call(functools.partial(spread, n, atom_rows), name='spread', ou...]
    pallas_call x1, Pallas kernels: 12.7 us -> 14.7 us  [shards(): pl.pallas_call(functools.partial(atoms, n, group), name='atoms', out_shap...]
    pallas_call x1, Pallas kernels: 8.25 us -> 10 us  [shards(): pl.pallas_call(functools.partial(merge, n), name='merge', out_shape=S((to...]
    dot_general x1, matrix products: 1.23 us -> 2.13 us  [shards(): jnp.dot(pooled, w_back, preferred_element_type=F32)]
where the time goes in v2:
time: 41.6 us; the launch traced here: 41.3 us
  Pallas kernels  38.5 us (93%)
  matrix products  2.13 us (5%)
  between operations  0.69 us (2%)
    pallas_call x1, Pallas kernels, shards(): pl.pallas_call(functools.partial(atoms, n, group), name='atoms', out_shap...  14.7 us
    pallas_call x1, Pallas kernels, shards(): pl.pallas_call(functools.partial(spread, n, atom_rows), name='spread', ou...  13.8 us
    pallas_call x1, Pallas kernels, shards(): pl.pallas_call(functools.partial(merge, n), name='merge', out_shape=S((to...  10 us
    dot_general x1, matrix products, shards(): jnp.dot(pooled, w_back, preferred_element_type=F32)  2.13 us

profile of v2, /device:TPU:0, one launch (start us, length us, event | category | flops | bytes accessed | tf_op | source)
XLA Modules:
  0.0 41.3 jit_solution(6229076257600674973)
XLA Ops:
  0.6 0.0 copy-start
  0.6 13.8 %spread.1 = (bf16[1920,128]{1,0:T(8,128)(2,1)}, bf16[96,128]{1,0:T(8,128)(2,1)}, s32[16,128]{1,0:T(8,128)}, s32[16,128]{1,0:T(8,128)}, s32[8,128]{1,0:T(8,128)}) custom-call(bf16[512,768]{1,0:T(8,128)(2,1)} %cond_hbm.1, bf16[768,128]{1,0:T(8,128)(2,1)} %wtok_hbm.1, bf16[4096,128]{1,0:T(8,128)(2,1)} %feat_hbm.1, s32[4,128]{1,0:T(4,128)} %bitcast.3), custom_call_target="tpu_custom_call" | custom-call | tf_op jit(solution)/shard_map/spread/pallas_call | solution.py:322
  14.5 0.0 copy-start.1
  14.5 14.7 %atoms.1 = (bf16[4096,128]{1,0:T(8,128)(2,1)}, f32[512,128]{1,0:T(8,128)}, bf16[2,512,128]{2,1,0:T(8,128)(2,1)}) custom-call(s32[8,128]{1,0:T(8,128)} %get-tuple-element.10.wins, bf16[1920,128]{1,0:T(8,128)(2,1)} %get-tuple-element.11.table, bf16[96,128]{1,0:T(8,128)(2,1)} %get-tuple-element.12.halo, bf16[4096,128]{1,0:T(8,128)(2,1)} %feat_hbm.1, ...), custom_call_target="tpu_custom_call" | custom-call | tf_op jit(solution)/shard_map/atoms/pallas_call | solution.py:341
  29.1 10.0 %merge.1 = bf16[512,128]{1,0:T(8,128)(2,1)} custom-call(f32[512,128]{1,0:T(8,128)} %get-tuple-element.15.own_ref, bf16[2,512,128]{2,1,0:T(8,128)(2,1)} %get-tuple-element.16.sides_ref, s32[4,128]{1,0:T(4,128)} %bitcast.4), custom_call_target="tpu_custom_call" | custom-call | tf_op jit(solution)/shard_map/merge/pallas_call | solution.py:358
  39.2 0.0 copy-done
  39.2 0.0 copy-done.1
  39.2 2.1 %add_convert_fusion = bf16[512,768]{1,0:T(8,128)(2,1)} fusion(bf16[512,768]{1,0:T(8,128)(2,1)S(1)} %copy-done.1, bf16[512,128]{1,0:T(8,128)(2,1)} %merge.1, bf16[128,768]{1,0:T(8,128)(2,1)S(1)} %copy-done), kind=kOutput, calls=%fused_computation | convolution fusion | flops 101842944 | bytes 1900544 | tf_op jit(solution)/shard_map/dot_general | solution.py:368
Async XLA Ops:
  0.6 38.5 %copy-start = (bf16[128,768]{1,0:T(8,128)(2,1)S(1)}, bf16[128,768]{1,0:T(8,128)(2,1)}, u32[]{:S(2)}) copy-start(bf16[128,768]{1,0:T(8,128)(2,1)} %param.17) | copy-start | bytes 589828
  14.5 24.7 %copy-start.1 = (bf16[512,768]{1,0:T(8,128)(2,1)S(1)}, bf16[512,768]{1,0:T(8,128)(2,1)}, u32[]{:S(2)}) copy-start(bf16[512,768]{1,0:T(8,128)(2,1)} %cond_hbm.1) | copy-start | bytes 2359300
